TPU v7x, 16 devices: a 4x2x1 block of a 4x4x8 slice. The times are simulated.
16 devices in a mesh: rep: 2 (over y, z), dp: 8 (over x, core).
Axes of the slice: x: 4, y: 2, z: 1, core: 2. Of those that a mesh axis runs over, the one named last changes fastest.
The devices are a block of a 4x4x8 slice.
Arguments:
- a: bfloat16 [16, 4, 2048, 1024], P(('rep', 'dp')), parts along dimension 0
- g: bfloat16 [16, 4, 2048, 3200], P(('rep', 'dp')), parts along dimension 0
Outputs:
- output: bfloat16 [8, 1024, 3200], P('rep'), parts along dimension 0
There are 2 independent parts. A program takes and returns all parts, laid end to end along the dimension named above; each array names one.
All inputs are finite; a program needn't handle non-finite values.
Results may differ from a plain program's by a relative error of at most 0.012.
Values are sent between devices in bfloat16 or wider.
A program may use at most 768 MiB of HBM per device.

v0:
```python
import jax
import jax.numpy as jnp


def solution(mesh):
    groups = mesh.shape["rep"]

    def step(a, g):
        a, g = (t.reshape(groups, -1, *t.shape[1:]) for t in (a, g))
        sums = jnp.einsum("rsntd,rsntf->rndf", a, g, preferred_element_type=jnp.float32)
        return sums.astype(jnp.bfloat16).reshape(-1, *sums.shape[2:])

    return step
```

profile of v0, /device:TPU:113, one launch (start us, length us, event | category | flops | bytes accessed | tf_op | source)
XLA Modules:
  0.0 593.8 jit_solution(7284460216555358982)
XLA Ops:
  0.0 69.9 %fusion.2 = f32[1,4,1024,3200]{3,2,1,0:T(8,128)} fusion(bf16[1,4,2048,3200]{3,2,1,0:T(8,128)(2,1)} %param.1, bf16[1,4,2048,1024]{3,2,1,0:T(8,128)(2,1)} %param), kind=kOutput, calls=%fused_computation.2 | convolution fusion | flops 53687091200 | bytes 121634816 | tf_op jit(solution)/rsntd,rsntf->rndf/dot_general | solution.py:10
  69.9 523.9 %all-reduce.2 = bf16[1,4,1024,3200]{3,2,1,0:T(8,128)(2,1)} all-reduce(f32[1,4,1024,3200]{3,2,1,0:T(8,128)} %fusion.2), channel_id=1, replica_groups=[2,8]<=[16], use_global_device_ids=true, to_apply=%add.clone | all-reduce | flops 13107200 | bytes 78643200 | tf_op jit(solution)/rsntd,rsntf->rndf/dot_general | solution.py:10
where the time goes:
time: 596 us; the launch traced here: 594 us
  blocking collectives  524 us (88%)
  matrix products  69.9 us (12%)
    dot_general x1, blocking collectives, step(): jnp.einsum('rsntd,rsntf->rndf', a, g, preferred_element_type=jnp.float32)  524 us
    dot_general x1, matrix products, step(): jnp.einsum('rsntd,rsntf->rndf', a, g, preferred_element_type=jnp.float32)  69.9 us

commit v1 on v0

v1 whole, which is shorter than its diff:
```python
import functools

import jax
import jax.numpy as jnp
from jax import lax
from jax.experimental import pallas as pl
from jax.experimental.pallas import tpu as pltpu
from jax.sharding import PartitionSpec as P

MESH = pl.DeviceIdType.MESH
CORES = 2
LEFT, RIGHT, MATE = 0, 1, 2
SLOTS = 8
F32, BF16 = jnp.float32, jnp.bfloat16


def kernel(
    chips, wide, a_hbm, g_hbm, out,
    a_buf, g_buf, mine, give, take, keep, ab_out, ab_in, c_out, c_in,
    a_sem, g_sem, give_sem, take_sem, ab_sent, ab_got, c_sent, c_got,
    own_sent, own_got, far_sent, far_got, fwd_sent, fwd_got,
):
    matrices, rows, columns = out.shape
    blocks = columns // wide
    units = matrices * blocks
    half = rows // CORES
    own = half // chips
    sub = own // 2

    me = lax.axis_index("dp")
    x, core = me // CORES, me % CORES
    xl, xr, opp = (x + chips - 1) % chips, (x + 1) % chips, (x + 2) % chips
    dev = {LEFT: xl * CORES + core, RIGHT: xr * CORES + core, MATE: x * CORES + 1 - core}
    base, mate_base = core * half, (1 - core) * half

    def load_a(n):
        return pltpu.make_async_copy(a_hbm.at[0, n], a_buf.at[n % 2], a_sem.at[n % 2])

    def load_g(u):
        return pltpu.make_async_copy(
            g_hbm.at[0, u // blocks, :, pl.ds(pl.multiple_of(u % blocks * wide, 128), wide)],
            g_buf.at[u % 2],
            g_sem.at[u % 2],
        )

    def remote(src, dst, sent, got, to):
        return pltpu.make_async_remote_copy(
            src_ref=src, dst_ref=dst, send_sem=sent, recv_sem=got,
            device_id={"dp": dev[to]}, device_id_type=MESH,
        )

    def place(u, row, count):
        return out.at[
            u // blocks,
            pl.ds(pl.multiple_of(row, sub), count),
            pl.ds(pl.multiple_of(u % blocks * wide, 128), wide),
        ]

    def hand(u):
        s = u % 4
        return remote(give.at[u % 2], take.at[s], give_sem.at[s], take_sem.at[s], MATE)

    def ab(u, to):
        s = u % SLOTS
        return remote(ab_out.at[u % 4, to], ab_in.at[s, to], ab_sent.at[s, to], ab_got.at[s, to], to)

    def c(u, to):
        s = u % SLOTS
        return remote(c_out.at[u % 4, to], c_in.at[s, to], c_sent.at[s, to], c_got.at[s, to], to)

    def owned(u, to):
        s, ref = u % SLOTS, place(u, base + x * own, own)
        return remote(ref, ref, own_sent.at[s, to], own_got.at[s, to], to)

    def far(u, to):
        s = u % SLOTS
        row = base + (xl * own if to == RIGHT else xr * own + sub)
        ref = place(u, row, sub)
        return remote(ref, ref, far_sent.at[s, to], far_got.at[s, to], to)

    def forward(u, k):
        s = u % SLOTS
        ref = place(u, base + (xl, xr, opp)[k] * own, own)
        return remote(ref, ref, fwd_sent.at[s, k], fwd_got.at[s, k], MATE)

    load_a(0).start()
    load_g(0).start()
    barrier = pltpu.get_barrier_semaphore()
    for to in (LEFT, RIGHT, MATE):
        pl.semaphore_signal(barrier, inc=1, device_id={"dp": dev[to]}, device_id_type=MESH)
    pl.semaphore_wait(barrier, 3)

    def multiply(u, row, count):
        return lax.dot_general(
            a_buf[u // blocks % 2, :, pl.ds(pl.multiple_of(row, 128), count)],
            g_buf[u % 2],
            (((0,), (0,)), ((), ())),
            preferred_element_type=F32,
        )

    def iteration(t, carry):
        def stage(lag):
            u = t - lag
            return u, pl.when((u >= 0) & (u < units))

        u_next, on_next = stage(-1)

        @on_next
        def _():
            load_g(u_next).start()

        @pl.when((t % blocks == 0) & (t // blocks + 1 < matrices))
        def _():
            load_a(t // blocks + 1).start()

        u_b, on_b = stage(1)

        @on_b
        def _():
            u, s, k = u_b, u_b % 4, u_b % 2
            hand(u).wait()

            @pl.when(u >= 4)
            def _():
                for to in (LEFT, RIGHT):
                    ab(u - 4, to).wait_send()

            def total(owner, offset):
                where = pl.ds(pl.multiple_of(owner * own + offset, sub), sub)
                return mine[k, where, :] + take[s, where, :].astype(F32)

            ab_out[s, LEFT, :sub, :] = total(opp, 0).astype(BF16)
            ab_out[s, LEFT, sub:, :] = total(xl, sub).astype(BF16)
            ab(u, LEFT).start()
            ab_out[s, RIGHT, :sub, :] = total(opp, sub).astype(BF16)
            ab_out[s, RIGHT, sub:, :] = total(xr, 0).astype(BF16)
            ab(u, RIGHT).start()
            keep[s, 0] = total(xl, 0)
            keep[s, 1] = total(xr, sub)
            keep[s, 2] = total(x, 0)
            keep[s, 3] = total(x, sub)

        u_c, on_c = stage(2)

        @on_c
        def _():
            u, s, r = u_c, u_c % 4, u_c % SLOTS

            @pl.when(u >= 4)
            def _():
                for to in (LEFT, RIGHT):
                    c(u - 4, to).wait_send()

            for to in (LEFT, RIGHT):
                ab(u, to).wait_recv()
                c_out[s, to] = (keep[s, to] + ab_in[r, to, :sub, :].astype(F32)).astype(BF16)
                c(u, to).start()

        u_d, on_d = stage(3)

        @on_d
        def _():
            u, s, r = u_d, u_d % 4, u_d % SLOTS
            cols = pl.ds(pl.multiple_of(u % blocks * wide, 128), wide)
            for k in (0, 1):
                c(u, k).wait_recv()
                total = keep[s, 2 + k] + c_in[r, k].astype(F32) + ab_in[r, 1 - k, sub:, :].astype(F32)
                row = pl.ds(pl.multiple_of(base + x * own + k * sub, sub), sub)
                out[u // blocks, row, cols] = total.astype(BF16)
            for to in (LEFT, RIGHT, MATE):
                owned(u, to).start()

        u_e, on_e = stage(4)

        @on_e
        def _():
            owned(u_e, RIGHT).wait_recv()
            far(u_e, RIGHT).start()
            owned(u_e, LEFT).wait_recv()
            far(u_e, LEFT).start()
            forward(u_e, 0).start()
            forward(u_e, 1).start()

        u_g, on_g = stage(5)

        @on_g
        def _():
            far(u_g, RIGHT).wait_recv()
            far(u_g, LEFT).wait_recv()
            forward(u_g, 2).start()

        u_h, on_h = stage(6)

        @on_h
        def _():
            for to in (LEFT, RIGHT, MATE):
                owned(u_h, to).wait_send()
            owned(u_h, MATE).wait_recv()
            for to in (LEFT, RIGHT):
                far(u_h, to).wait_send()
            for k in range(3):
                forward(u_h, k).wait()

        u_a, on_a = stage(0)

        @on_a
        def _():
            u = u_a

            @pl.when(u % blocks == 0)
            def _():
                load_a(u // blocks).wait()

            load_g(u).wait()

            @pl.loop(0, half, step=256)
            def _(i):
                give[u % 2, pl.ds(pl.multiple_of(i, 256), 256), :] = multiply(u, mate_base + i, 256).astype(BF16)

            hand(u).start()

            @pl.loop(0, half, step=256)
            def _(i):
                mine[u % 2, pl.ds(pl.multiple_of(i, 256), 256), :] = multiply(u, base + i, 256)

        return carry

    lax.fori_loop(0, units + 7, iteration, 0)
    for i in range(4):
        for to in (LEFT, RIGHT):
            ab(units - 4 + i, to).wait_send()
            c(units - 4 + i, to).wait_send()


def solution(mesh):
    chips = mesh.shape["dp"] // CORES

    def device(a, g):
        _, matrices, tokens, rows = a.shape
        columns = g.shape[-1]
        wide = 128 * next(k for k in (5, 6, 4, 3, 2, 1) if columns % (128 * k) == 0)
        half = rows // CORES
        own = half // chips
        sub = own // 2
        dma = pltpu.SemaphoreType.DMA
        sums = pl.pallas_call(
            functools.partial(kernel, chips, wide),
            out_shape=pltpu.VMEM((matrices, rows, columns), BF16),
            in_specs=[pl.BlockSpec(memory_space=pltpu.HBM)] * 2,
            out_specs=pl.BlockSpec(memory_space=pltpu.VMEM),
            scratch_shapes=[
                pltpu.VMEM((2, tokens, rows), BF16),
                pltpu.VMEM((2, tokens, wide), BF16),
                pltpu.VMEM((2, half, wide), F32),
                pltpu.VMEM((2, half, wide), BF16),
                pltpu.VMEM((4, half, wide), BF16),
                pltpu.VMEM((4, 4, sub, wide), F32),
                pltpu.VMEM((4, 2, own, wide), BF16),
                pltpu.VMEM((SLOTS, 2, own, wide), BF16),
                pltpu.VMEM((4, 2, sub, wide), BF16),
                pltpu.VMEM((SLOTS, 2, sub, wide), BF16),
                dma((2,)), dma((2,)), dma((4,)), dma((4,)),
                dma((SLOTS, 2)), dma((SLOTS, 2)), dma((SLOTS, 2)), dma((SLOTS, 2)),
                dma((SLOTS, 3)), dma((SLOTS, 3)), dma((SLOTS, 2)), dma((SLOTS, 2)),
                dma((SLOTS, 3)), dma((SLOTS, 3)),
            ],
            compiler_params=pltpu.CompilerParams(
                collective_id=0, has_side_effects=True, vmem_limit_bytes=37 * 2**20
            ),
            cost_estimate=pl.CostEstimate(
                flops=2 * matrices * tokens * rows * columns,
                bytes_accessed=2 * matrices * tokens * (rows + columns),
                transcendentals=0,
            ),
        )(a, g)

        def store(held, result, sem):
            copies = [pltpu.make_async_copy(held.at[n], result.at[n], sem.at[n]) for n in range(matrices)]
            for copy in copies:
                copy.start()
            for copy in copies:
                copy.wait()

        return pl.pallas_call(
            store,
            out_shape=jax.ShapeDtypeStruct(sums.shape, BF16),
            in_specs=[pl.BlockSpec(memory_space=pltpu.VMEM)],
            out_specs=pl.BlockSpec(memory_space=pltpu.HBM),
            scratch_shapes=[dma((matrices,))],
            compiler_params=pltpu.CompilerParams(vmem_limit_bytes=2**20),
        )(pltpu.with_memory_space_constraint(sums, pltpu.VMEM))

    return jax.shard_map(
        device, mesh=mesh, in_specs=(P(("rep", "dp")), P(("rep", "dp"))), out_specs=P("rep"), check_vma=False
    )
```

time: 596 us -> 237 us (0.40)
  blocking collectives: 524 us -> 0 us
  Pallas kernels: 0 us -> 237 us
  matrix products: 69.9 us -> 0 us
    dot_general x1 -> x0, blocking collectives: 524 us -> none  [step(): jnp.einsum('rsntd,rsntf->rndf', a, g, preferred_element_type=jnp.float32)]
    pallas_call x0 -> x2, Pallas kernels: none -> 237 us  [the longest x1 228 us: device(): pl.pallas_call(functools.partial(kernel, chips, wide), out_shape=pltpu.VM...]
    dot_general x1 -> x0, matrix products: 69.9 us -> none  [step(): jnp.einsum('rsntd,rsntf->rndf', a, g, preferred_element_type=jnp.float32)]
where the time goes in v1:
time: 237 us
  Pallas kernels  237 us (100%)
    pallas_call x1, Pallas kernels, device(): pl.pallas_call(functools.partial(kernel, chips, wide), out_shape=pltpu.VM...  228 us
    pallas_call x1, Pallas kernels, device(): pl.pallas_call(store, out_shape=jax.ShapeDtypeStruct(sums.shape, BF16), i...  8.92 us

profile of v1, /device:TPU:113, one launch (start us, length us, event | category | flops | bytes accessed | tf_op | source)
XLA Modules:
  0.0 236.6 jit_solution(14729742409938741092)
XLA Ops:
  0.0 227.7 %shard_map.28.held = bf16[4,1024,3200]{2,1,0:T(8,128)(2,1)S(1)} custom-call(bf16[1,4,2048,1024]{3,2,1,0:T(8,128)(2,1)} %a_hbm.1, bf16[1,4,2048,3200]{3,2,1,0:T(8,128)(2,1)} %g_hbm.1), custom_call_target="tpu_custom_call" | custom-call | flops 53687091200 | bytes 69206016 | tf_op jit(solution)/shard_map/pallas_call | solution.py:246
  227.7 8.9 %shard_map.29 = bf16[4,1024,3200]{2,1,0:T(8,128)(2,1)} custom-call(bf16[4,1024,3200]{2,1,0:T(8,128)(2,1)S(1)} %shard_map.28.held), custom_call_target="tpu_custom_call" | custom-call | tf_op jit(solution)/shard_map/pallas_call | solution.py:284

commit v2 on v0

v2 whole, which is shorter than its diff:
```python
import functools

import jax
import jax.numpy as jnp
from jax import lax
from jax.experimental import pallas as pl
from jax.experimental.pallas import tpu as pltpu
from jax.sharding import PartitionSpec as P

MESH = pl.DeviceIdType.MESH
CORES = 2
LEFT, RIGHT, MATE = 0, 1, 2
SLOTS = 5
TILE = 512
LAG = 2
F32, BF16 = jnp.float32, jnp.bfloat16


def cut(columns):
    blocks = max(columns // TILE, 1)
    return blocks, blocks // 2, columns - (blocks - 1) * TILE


def kernel(
    chips, a_hbm, g_hbm, out,
    a_buf, g_buf, mine, give, take, keep, ab_out, ab_in, c_out, c_in,
    a_sem, g_sem, give_sem, take_sem, ab_sent, ab_got, c_sent, c_got,
    own_got, far_got, out_sent, mate_sent, mate_got,
):
    matrices, rows, columns = out.shape
    blocks, middle, wide = cut(columns)
    units = matrices * blocks
    half = rows // CORES
    own = half // chips
    sub = own // 2

    me = lax.axis_index("dp")
    x, core = me // CORES, me % CORES
    xl, xr, opp = (x + chips - 1) % chips, (x + 1) % chips, (x + 2) % chips
    dev = {LEFT: xl * CORES + core, RIGHT: xr * CORES + core, MATE: x * CORES + 1 - core}
    base, mate_base = core * half, (1 - core) * half

    def columns_of(u, w):
        j = u % blocks
        return pl.ds(pl.multiple_of(j * TILE + (j + blocks - 1 - middle) // blocks * (wide - TILE), 128), w)

    def load_a(n, h):
        where = pl.ds(pl.multiple_of((mate_base, base)[h], 128), half)
        return pltpu.make_async_copy(a_hbm.at[0, n, :, where], a_buf.at[n % 2, h], a_sem.at[h])

    def load_g(u, w):
        return pltpu.make_async_copy(
            g_hbm.at[0, u // blocks, :, columns_of(u, w)], g_buf.at[u % 2, :, pl.ds(0, w)], g_sem.at[u % 2]
        )

    def remote(src, dst, sent, got, to):
        return pltpu.make_async_remote_copy(
            src_ref=src, dst_ref=dst, send_sem=sent, recv_sem=got,
            device_id={"dp": dev[to]}, device_id_type=MESH,
        )

    def place(u, w, row, count):
        return out.at[u // blocks, pl.ds(pl.multiple_of(row, sub), count), columns_of(u, w)]

    def hand(u, w):
        s, cols = u % 2, pl.ds(0, w)
        return remote(give.at[s, :, cols], take.at[s, :, cols], give_sem.at[s], take_sem.at[s], MATE)

    def ab(u, w, to):
        s, k, cols = u % SLOTS, u % 2, pl.ds(0, w)
        return remote(ab_out.at[k, to, :, cols], ab_in.at[s, to, :, cols], ab_sent.at[k], ab_got.at[s, to], to)

    def c(u, w, to):
        s, k, cols = u % SLOTS, u % 2, pl.ds(0, w)
        return remote(c_out.at[k, to, :, cols], c_in.at[s, to, :, cols], c_sent.at[k], c_got.at[s], to)

    def owned(u, w, to):
        s, ref = u % SLOTS, place(u, w, base + x * own, own)
        if to == MATE:
            return remote(ref, ref, mate_sent, mate_got, to)
        return remote(ref, ref, out_sent, own_got.at[s, to], to)

    def far(u, w, to):
        row = base + (xl * own if to == RIGHT else xr * own + sub)
        ref = place(u, w, row, sub)
        return remote(ref, ref, out_sent, far_got.at[u % SLOTS], to)

    def forward(u, w, k):
        ref = place(u, w, base + (xl, xr, opp)[k] * own, own)
        return remote(ref, ref, mate_sent, mate_got, MATE)

    def wait_for(ref, sem):
        pltpu.make_async_copy(ref, ref, sem).wait()

    def run(stage, u, also=True):
        here = (u >= 0) & (u < units) & also
        if wide == TILE:
            pl.when(here)(lambda: stage(u, TILE))
        else:
            pl.when(here & (u % blocks != middle))(lambda: stage(u, TILE))
            pl.when(here & (u % blocks == middle))(lambda: stage(u, wide))

    def multiply(u, w, h):
        return lax.dot_general(
            a_buf[u // blocks % 2, h],
            g_buf[u % 2, :, :w],
            (((0,), (0,)), ((), ())),
            preferred_element_type=F32,
        )

    def stage_a(u, w):
        load_g(u, w).wait()
        give[u % 2, :, :w] = multiply(u, w, 0).astype(BF16)

    def stage_a2(u, w):
        hand(u, w).start()
        mine[:, :w] = multiply(u, w, 1)

    def stage_b(u, w):
        k = u % 2
        hand(u, w).wait()

        def total(owner, offset):
            where = pl.ds(pl.multiple_of(owner * own + offset, sub), sub)
            return mine[where, :w] + take[k, where, :w].astype(F32)

        ab_out[k, LEFT, :sub, :w] = total(opp, 0).astype(BF16)
        ab_out[k, LEFT, sub:, :w] = total(xl, sub).astype(BF16)
        ab(u, w, LEFT).start()
        ab_out[k, RIGHT, :sub, :w] = total(opp, sub).astype(BF16)
        ab_out[k, RIGHT, sub:, :w] = total(xr, 0).astype(BF16)
        ab(u, w, RIGHT).start()
        s = u % SLOTS
        keep[s, 0, :, :w] = total(xl, 0)
        keep[s, 1, :, :w] = total(xr, sub)
        keep[s, 2, :, :w] = total(x, 0)
        keep[s, 3, :, :w] = total(x, sub)

    def stage_b0(u, w):
        wait_for(ab_out.at[u % 2, :, :, pl.ds(0, w)], ab_sent.at[u % 2])

    def stage_c(u, w):
        s, k = u % SLOTS, u % 2
        for to in (LEFT, RIGHT):
            ab(u, w, to).wait_recv()
            c_out[k, to, :, :w] = (keep[s, to, :, :w] + ab_in[s, to, :sub, :w].astype(F32)).astype(BF16)
            c(u, w, to).start()
        for to in (LEFT, RIGHT):
            keep[s, 3 - to, :, :w] += ab_in[s, to, sub:, :w].astype(F32)

    def stage_c0(u, w):
        wait_for(c_out.at[u % 2, :, :, pl.ds(0, w)], c_sent.at[u % 2])

    def stage_d(u, w):
        s = u % SLOTS
        wait_for(c_in.at[s, :, :, pl.ds(0, w)], c_got.at[s])
        for k in (0, 1):
            total = keep[s, 2 + k, :, :w] + c_in[s, k, :, :w].astype(F32)
            row = pl.ds(pl.multiple_of(base + x * own + k * sub, sub), sub)
            out[u // blocks, row, columns_of(u, w)] = total.astype(BF16)
        for to in (LEFT, RIGHT, MATE):
            owned(u, w, to).start()

    def stage_e(u, w):
        owned(u, w, RIGHT).wait_recv()
        far(u, w, RIGHT).start()
        owned(u, w, LEFT).wait_recv()
        far(u, w, LEFT).start()
        forward(u, w, 0).start()
        forward(u, w, 1).start()

    def stage_g(u, w):
        wait_for(place(u, w, base + opp * own, own), far_got.at[u % SLOTS])
        forward(u, w, 2).start()

    barrier = pltpu.get_barrier_semaphore()
    load_a(0, 0).start()
    load_g(0, TILE).start()
    load_a(0, 1).start()
    for to in (LEFT, RIGHT, MATE):
        pl.semaphore_signal(barrier, inc=1, device_id={"dp": dev[to]}, device_id_type=MESH)

    def iteration(t, carry):
        n, first = t // blocks, (t % blocks == 0) & (t < units)
        run(lambda u, w: load_g(u, w).start(), t + 1)

        @pl.when((t % blocks == 1) & (n + 1 < matrices))
        def _():
            for h in (0, 1):
                load_a(n + 1, h).start()

        pl.when(first)(lambda: load_a(n, 0).wait())
        run(stage_a, t)
        pl.when(t == 0)(lambda: pl.semaphore_wait(barrier, 3))
        pl.when(first)(lambda: load_a(n, 1).wait())
        run(stage_a2, t)
        run(stage_b0, t - 2)
        run(stage_b, t)
        run(stage_c0, t - 2 - LAG)
        run(stage_c, t - LAG)
        run(stage_d, t - LAG - 1)
        run(stage_e, t - LAG - 2)
        run(stage_g, t - LAG - 3)
        return carry

    lax.fori_loop(0, units + LAG + 3, iteration, 0)
    wait_for(out.at[:, pl.ds(pl.multiple_of(base, half), half), :], mate_sent)
    wait_for(out.at[:, pl.ds(0, 3 * own), :], out_sent)
    wait_for(out.at[:, pl.ds(pl.multiple_of(mate_base, half), half), :], mate_got)


def solution(mesh):
    chips = mesh.shape["dp"] // CORES

    def device(a, g):
        _, matrices, tokens, rows = a.shape
        columns = g.shape[-1]
        wide = cut(columns)[2]
        half = rows // CORES
        own = half // chips
        sub = own // 2
        dma = pltpu.SemaphoreType.DMA
        sums = pl.pallas_call(
            functools.partial(kernel, chips),
            out_shape=pltpu.VMEM((matrices, rows, columns), BF16),
            in_specs=[pl.BlockSpec(memory_space=pltpu.HBM)] * 2,
            out_specs=pl.BlockSpec(memory_space=pltpu.VMEM),
            scratch_shapes=[
                pltpu.VMEM((2, CORES, tokens, half), BF16),
                pltpu.VMEM((2, tokens, wide), BF16),
                pltpu.VMEM((half, wide), F32),
                pltpu.VMEM((2, half, wide), BF16),
                pltpu.VMEM((2, half, wide), BF16),
                pltpu.VMEM((SLOTS, 4, sub, wide), F32),
                pltpu.VMEM((2, 2, own, wide), BF16),
                pltpu.VMEM((SLOTS, 2, own, wide), BF16),
                pltpu.VMEM((2, 2, sub, wide), BF16),
                pltpu.VMEM((SLOTS, 2, sub, wide), BF16),
                dma((2,)), dma((2,)), dma((2,)), dma((2,)), dma((2,)), dma((SLOTS, 2)), dma((2,)), dma((SLOTS,)),
                dma((SLOTS, 2)), dma((SLOTS,)), dma, dma, dma,
            ],
            compiler_params=pltpu.CompilerParams(
                collective_id=0, has_side_effects=True, vmem_limit_bytes=37 * 2**20
            ),
            cost_estimate=pl.CostEstimate(
                flops=2 * matrices * tokens * rows * columns,
                bytes_accessed=2 * matrices * tokens * (rows + columns),
                transcendentals=0,
            ),
        )(a, g)

        def store(held, result, sem):
            copies = [pltpu.make_async_copy(held.at[n], result.at[n], sem.at[n]) for n in range(matrices)]
            for copy in copies:
                copy.start()
            for copy in copies:
                copy.wait()

        return pl.pallas_call(
            store,
            out_shape=jax.ShapeDtypeStruct(sums.shape, BF16),
            in_specs=[pl.BlockSpec(memory_space=pltpu.VMEM)],
            out_specs=pl.BlockSpec(memory_space=pltpu.HBM),
            scratch_shapes=[dma((matrices,))],
            compiler_params=pltpu.CompilerParams(vmem_limit_bytes=2**20),
        )(pltpu.with_memory_space_constraint(sums, pltpu.VMEM))

    return jax.shard_map(
        device, mesh=mesh, in_specs=(P(("rep", "dp")), P(("rep", "dp"))), out_specs=P("rep"), check_vma=False
    )
```

time: 596 us -> 233 us (0.39)
  blocking collectives: 524 us -> 0 us
  Pallas kernels: 0 us -> 233 us
  matrix products: 69.9 us -> 0 us
    dot_general x1 -> x0, blocking collectives: 524 us -> none  [step(): jnp.einsum('rsntd,rsntf->rndf', a, g, preferred_element_type=jnp.float32)]
    pallas_call x0 -> x2, Pallas kernels: none -> 233 us  [the longest x1 224 us: device(): pl.pallas_call(functools.partial(kernel, chips), out_shape=pltpu.VMEM((ma...]
    dot_general x1 -> x0, matrix products: 69.9 us -> none  [step(): jnp.einsum('rsntd,rsntf->rndf', a, g, preferred_element_type=jnp.float32)]
where the time goes in v2:
time: 233 us
  Pallas kernels  233 us (100%)
    pallas_call x1, Pallas kernels, device(): pl.pallas_call(functools.partial(kernel, chips), out_shape=pltpu.VMEM((ma...  224 us
    pallas_call x1, Pallas kernels, device(): pl.pallas_call(store, out_shape=jax.ShapeDtypeStruct(sums.shape, BF16), i...  8.92 us

profile of v2, /device:TPU:113, one launch (start us, length us, event | category | flops | bytes accessed | tf_op | source)
XLA Modules:
  0.0 233.0 jit_solution(16838494267431913326)
XLA Ops:
  0.0 224.1 %shard_map.28.held = bf16[4,1024,3200]{2,1,0:T(8,128)(2,1)S(1)} custom-call(bf16[1,4,2048,1024]{3,2,1,0:T(8,128)(2,1)} %a_hbm.1, bf16[1,4,2048,3200]{3,2,1,0:T(8,128)(2,1)} %g_hbm.1), custom_call_target="tpu_custom_call" | custom-call | flops 53687091200 | bytes 69206016 | tf_op jit(solution)/shard_map/pallas_call | solution.py:223
  224.1 8.9 %shard_map.29 = bf16[4,1024,3200]{2,1,0:T(8,128)(2,1)} custom-call(bf16[4,1024,3200]{2,1,0:T(8,128)(2,1)S(1)} %shard_map.28.held), custom_call_target="tpu_custom_call" | custom-call | tf_op jit(solution)/shard_map/pallas_call | solution.py:259

commit v3 on v2

--- a/solution.py
+++ b/solution.py
@@ -12,7 +12,6 @@
 LEFT, RIGHT, MATE = 0, 1, 2
 SLOTS = 5
 TILE = 512
-LAG = 2
 F32, BF16 = jnp.float32, jnp.bfloat16
 
 
@@ -28,6 +27,7 @@
     own_got, far_got, out_sent, mate_sent, mate_got,
 ):
     matrices, rows, columns = out.shape
+    tokens = a_hbm.shape[2]
     blocks, middle, wide = cut(columns)
     units = matrices * blocks
     half = rows // CORES
@@ -51,6 +51,16 @@
     def load_g(u, w):
         return pltpu.make_async_copy(
             g_hbm.at[0, u // blocks, :, columns_of(u, w)], g_buf.at[u % 2, :, pl.ds(0, w)], g_sem.at[u % 2]
+        )
+
+    def load_first(k):
+        part = pl.ds(k * (tokens // 2), tokens // 2)
+        where = pl.ds(pl.multiple_of(mate_base, 128), half)
+        return (
+            pltpu.make_async_copy(a_hbm.at[0, 0, part, where], a_buf.at[0, 0, part], a_sem.at[2 * k]),
+            pltpu.make_async_copy(
+                g_hbm.at[0, 0, part, pl.ds(0, TILE)], g_buf.at[0, part, pl.ds(0, TILE)], g_sem.at[2 * k]
+            ),
         )
 
     def remote(src, dst, sent, got, to):
@@ -100,10 +110,14 @@
             pl.when(here & (u % blocks != middle))(lambda: stage(u, TILE))
             pl.when(here & (u % blocks == middle))(lambda: stage(u, wide))
 
-    def multiply(u, w, h):
+    def run_late(stage, u):
+        run(stage, u, u < units - 1)
+        run(stage, units - 1, u == units - 2)
+
+    def multiply(u, w, h, start=0, end=tokens):
         return lax.dot_general(
-            a_buf[u // blocks % 2, h],
-            g_buf[u % 2, :, :w],
+            a_buf[u // blocks % 2, h, start:end],
+            g_buf[u % 2, start:end, :w],
             (((0,), (0,)), ((), ())),
             preferred_element_type=F32,
         )
@@ -174,11 +188,19 @@
         forward(u, w, 2).start()
 
     barrier = pltpu.get_barrier_semaphore()
-    load_a(0, 0).start()
-    load_g(0, TILE).start()
+    for k in (0, 1):
+        for copy in load_first(k):
+            copy.start()
     load_a(0, 1).start()
     for to in (LEFT, RIGHT, MATE):
         pl.semaphore_signal(barrier, inc=1, device_id={"dp": dev[to]}, device_id_type=MESH)
+    for copy in load_first(0):
+        copy.wait()
+    mine[:, :TILE] = multiply(0, TILE, 0, 0, tokens // 2)
+    for copy in load_first(1):
+        copy.wait()
+    give[0, :, :TILE] = (mine[:, :TILE] + multiply(0, TILE, 0, tokens // 2)).astype(BF16)
+    pl.semaphore_wait(barrier, 3)
 
     def iteration(t, carry):
         n, first = t // blocks, (t % blocks == 0) & (t < units)
@@ -189,21 +211,21 @@
             for h in (0, 1):
                 load_a(n + 1, h).start()
 
-        pl.when(first)(lambda: load_a(n, 0).wait())
-        run(stage_a, t)
-        pl.when(t == 0)(lambda: pl.semaphore_wait(barrier, 3))
+        pl.when(first & (t > 0))(lambda: load_a(n, 0).wait())
+        run(stage_a, t, t > 0)
         pl.when(first)(lambda: load_a(n, 1).wait())
         run(stage_a2, t)
+        run(stage_c0, t - 4, t - 4 != units - 3)
+        run(stage_c0, units - 3, t == units)
+        run_late(stage_c, t - 2)
         run(stage_b0, t - 2)
         run(stage_b, t)
-        run(stage_c0, t - 2 - LAG)
-        run(stage_c, t - LAG)
-        run(stage_d, t - LAG - 1)
-        run(stage_e, t - LAG - 2)
-        run(stage_g, t - LAG - 3)
+        run_late(stage_d, t - 3)
+        run_late(stage_e, t - 4)
+        run_late(stage_g, t - 5)
         return carry
 
-    lax.fori_loop(0, units + LAG + 3, iteration, 0)
+    lax.fori_loop(0, units + 4, iteration, 0)
     wait_for(out.at[:, pl.ds(pl.multiple_of(base, half), half), :], mate_sent)
     wait_for(out.at[:, pl.ds(0, 3 * own), :], out_sent)
     wait_for(out.at[:, pl.ds(pl.multiple_of(mate_base, half), half), :], mate_got)
@@ -236,7 +258,7 @@
                 pltpu.VMEM((SLOTS, 2, own, wide), BF16),
                 pltpu.VMEM((2, 2, sub, wide), BF16),
                 pltpu.VMEM((SLOTS, 2, sub, wide), BF16),
-                dma((2,)), dma((2,)), dma((2,)), dma((2,)), dma((2,)), dma((SLOTS, 2)), dma((2,)), dma((SLOTS,)),
+                dma((3,)), dma((3,)), dma((2,)), dma((2,)), dma((2,)), dma((SLOTS, 2)), dma((2,)), dma((SLOTS,)),
                 dma((SLOTS, 2)), dma((SLOTS,)), dma, dma, dma,
             ],
             compiler_params=pltpu.CompilerParams(

time: 233 us -> 232 us (level)
  no operation moved by 1% of the time
where the time goes in v3:
time: 232 us
  Pallas kernels  232 us (100%)
    pallas_call x1, Pallas kernels, device(): pl.pallas_call(functools.partial(kernel, chips), out_shape=pltpu.VMEM((ma...  223 us
    pallas_call x1, Pallas kernels, device(): pl.pallas_call(store, out_shape=jax.ShapeDtypeStruct(sums.shape, BF16), i...  8.92 us

profile of v3, /device:TPU:113, one launch (start us, length us, event | category | flops | bytes accessed | tf_op | source)
XLA Modules:
  0.0 231.9 jit_solution(17256234808384938105)
XLA Ops:
  0.0 223.0 %shard_map.28.held = bf16[4,1024,3200]{2,1,0:T(8,128)(2,1)S(1)} custom-call(bf16[1,4,2048,1024]{3,2,1,0:T(8,128)(2,1)} %a_hbm.1, bf16[1,4,2048,3200]{3,2,1,0:T(8,128)(2,1)} %g_hbm.1), custom_call_target="tpu_custom_call" | custom-call | flops 53687091200 | bytes 69206016 | tf_op jit(solution)/shard_map/pallas_call | solution.py:245
  223.0 8.9 %shard_map.29 = bf16[4,1024,3200]{2,1,0:T(8,128)(2,1)} custom-call(bf16[4,1024,3200]{2,1,0:T(8,128)(2,1)S(1)} %shard_map.28.held), custom_call_target="tpu_custom_call" | custom-call | tf_op jit(solution)/shard_map/pallas_call | solution.py:281

commit v4 on v3

--- a/solution.py
+++ b/solution.py
@@ -17,7 +17,7 @@
 
 def cut(columns):
     blocks = max(columns // TILE, 1)
-    return blocks, blocks // 2, columns - (blocks - 1) * TILE
+    return blocks, 2 * blocks // 3, columns - (blocks - 1) * TILE
 
 
 def kernel(
@@ -28,7 +28,7 @@
 ):
     matrices, rows, columns = out.shape
     tokens = a_hbm.shape[2]
-    blocks, middle, wide = cut(columns)
+    blocks, fat, wide = cut(columns)
     units = matrices * blocks
     half = rows // CORES
     own = half // chips
@@ -42,7 +42,7 @@
 
     def columns_of(u, w):
         j = u % blocks
-        return pl.ds(pl.multiple_of(j * TILE + (j + blocks - 1 - middle) // blocks * (wide - TILE), 128), w)
+        return pl.ds(pl.multiple_of(j * TILE + (j + blocks - 1 - fat) // blocks * (wide - TILE), 128), w)
 
     def load_a(n, h):
         where = pl.ds(pl.multiple_of((mate_base, base)[h], 128), half)
@@ -107,8 +107,8 @@
         if wide == TILE:
             pl.when(here)(lambda: stage(u, TILE))
         else:
-            pl.when(here & (u % blocks != middle))(lambda: stage(u, TILE))
-            pl.when(here & (u % blocks == middle))(lambda: stage(u, wide))
+            pl.when(here & (u % blocks != fat))(lambda: stage(u, TILE))
+            pl.when(here & (u % blocks == fat))(lambda: stage(u, wide))
 
     def run_late(stage, u):
         run(stage, u, u < units - 1)
@@ -272,7 +272,8 @@
         )(a, g)
 
         def store(held, result, sem):
-            copies = [pltpu.make_async_copy(held.at[n], result.at[n], sem.at[n]) for n in range(matrices)]
+            parts = [(n, pl.ds(k * half // 2, half // 2)) for n in range(matrices) for k in range(2 * rows // half)]
+            copies = [pltpu.make_async_copy(held.at[p], result.at[p], sem.at[i]) for i, p in enumerate(parts)]
             for copy in copies:
                 copy.start()
             for copy in copies:
@@ -283,7 +284,7 @@
             out_shape=jax.ShapeDtypeStruct(sums.shape, BF16),
             in_specs=[pl.BlockSpec(memory_space=pltpu.VMEM)],
             out_specs=pl.BlockSpec(memory_space=pltpu.HBM),
-            scratch_shapes=[dma((matrices,))],
+            scratch_shapes=[dma((matrices * 2 * rows // half,))],
             compiler_params=pltpu.CompilerParams(vmem_limit_bytes=2**20),
         )(pltpu.with_memory_space_constraint(sums, pltpu.VMEM))
 

time: 232 us -> 232 us (level)
  no operation moved by 1% of the time
where the time goes in v4:
time: 232 us
  Pallas kernels  232 us (100%)
    pallas_call x1, Pallas kernels, device(): pl.pallas_call(functools.partial(kernel, chips), out_shape=pltpu.VMEM((ma...  223 us
    pallas_call x1, Pallas kernels, device(): pl.pallas_call(store, out_shape=jax.ShapeDtypeStruct(sums.shape, BF16), i...  8.84 us

profile of v4, /device:TPU:113, one launch (start us, length us, event | category | flops | bytes accessed | tf_op | source)
XLA Modules:
  0.0 231.6 jit_solution(3960852576418287420)
XLA Ops:
  0.0 222.8 %shard_map.28.held = bf16[4,1024,3200]{2,1,0:T(8,128)(2,1)S(1)} custom-call(bf16[1,4,2048,1024]{3,2,1,0:T(8,128)(2,1)} %a_hbm.1, bf16[1,4,2048,3200]{3,2,1,0:T(8,128)(2,1)} %g_hbm.1), custom_call_target="tpu_custom_call" | custom-call | flops 53687091200 | bytes 69206016 | tf_op jit(solution)/shard_map/pallas_call | solution.py:245
  222.8 8.8 %shard_map.29 = bf16[4,1024,3200]{2,1,0:T(8,128)(2,1)} custom-call(bf16[4,1024,3200]{2,1,0:T(8,128)(2,1)S(1)} %shard_map.28.held), custom_call_target="tpu_custom_call" | custom-call | tf_op jit(solution)/shard_map/pallas_call | solution.py:282

commit v5 on v4

--- a/solution.py
+++ b/solution.py
@@ -273,18 +273,16 @@
 
         def store(held, result, sem):
             parts = [(n, pl.ds(k * half // 2, half // 2)) for n in range(matrices) for k in range(2 * rows // half)]
-            copies = [pltpu.make_async_copy(held.at[p], result.at[p], sem.at[i]) for i, p in enumerate(parts)]
-            for copy in copies:
-                copy.start()
-            for copy in copies:
-                copy.wait()
+            for p in parts:
+                pltpu.make_async_copy(held.at[p], result.at[p], sem).start()
+            pltpu.make_async_copy(held, result, sem).wait()
 
         return pl.pallas_call(
             store,
             out_shape=jax.ShapeDtypeStruct(sums.shape, BF16),
             in_specs=[pl.BlockSpec(memory_space=pltpu.VMEM)],
             out_specs=pl.BlockSpec(memory_space=pltpu.HBM),
-            scratch_shapes=[dma((matrices * 2 * rows // half,))],
+            scratch_shapes=[dma],
             compiler_params=pltpu.CompilerParams(vmem_limit_bytes=2**20),
         )(pltpu.with_memory_space_constraint(sums, pltpu.VMEM))
 

time: 232 us -> 232 us (level)
  no operation moved by 1% of the time
where the time goes in v5:
time: 232 us; the launch traced here: 231 us
  Pallas kernels  231 us (100%)
    pallas_call x1, Pallas kernels, device(): pl.pallas_call(functools.partial(kernel, chips), out_shape=pltpu.VMEM((ma...  223 us
    pallas_call x1, Pallas kernels, device(): pl.pallas_call(store, out_shape=jax.ShapeDtypeStruct(sums.shape, BF16), i...  8.7 us

profile of v5, /device:TPU:113, one launch (start us, length us, event | category | flops | bytes accessed | tf_op | source)
XLA Modules:
  0.0 231.5 jit_solution(17584652103371058003)
XLA Ops:
  0.0 222.8 %shard_map.28.held = bf16[4,1024,3200]{2,1,0:T(8,128)(2,1)S(1)} custom-call(bf16[1,4,2048,1024]{3,2,1,0:T(8,128)(2,1)} %a_hbm.1, bf16[1,4,2048,3200]{3,2,1,0:T(8,128)(2,1)} %g_hbm.1), custom_call_target="tpu_custom_call" | custom-call | flops 53687091200 | bytes 69206016 | tf_op jit(solution)/shard_map/pallas_call | solution.py:245
  222.8 8.7 %shard_map.29 = bf16[4,1024,3200]{2,1,0:T(8,128)(2,1)} custom-call(bf16[4,1024,3200]{2,1,0:T(8,128)(2,1)S(1)} %shard_map.28.held), custom_call_target="tpu_custom_call" | custom-call | tf_op jit(solution)/shard_map/pallas_call | solution.py:280
